TPU v7x, 512 devices: a whole 4x8x8 slice. The times are simulated.
512 devices in a mesh: freq: 2 (over x_hi), base: 16 (over x_lo, y), pix: 16 (over z, core).
Axes of the slice: x: 4 (x_hi: 2, x_lo: 2; x = x_hi * 2 + x_lo), y: 8, z: 8, core: 2. Of those that a mesh axis runs over, the one named last changes fastest.
Arguments:
- sensing_operator_parts: bfloat16 [2, 16384, 32768], P('freq', 'base', 'pix'), may hold values from -1 to 1
- sampled_correlations: float32 [64, 16384], P('freq', 'base'), may hold values from -40 to 40
- first_sky_estimate: float32 [64, 16, 16, 128], P('freq', 'pix', 'base'), may hold values from -2.5 to 2.5
- patch_order_record: int32 [6, 256], P(None, 'pix'), may hold values from 0 to 255, as said below
Outputs:
- image: float32 [64, 16, 16, 128], P('freq', 'pix', 'base')
Inputs may be any that keep to these rules, and one draw needn't show every extreme that they name: `patch_order_record`: each row holds every tile number once; the tiles of rank under 64 are the same in every row.
All inputs are finite; a program needn't handle non-finite values.
Results may differ from a plain program's by a relative error of at most 0.0014.
Values may be sent and summed in bfloat16 or wider, within the bound.
A program may use at most 64 MiB of HBM per device.

v0:
```python
import jax
import jax.numpy as jnp
from jax import lax
from jax.sharding import PartitionSpec as P

CH = 64
TILE = 128
ITERS = 6


descent_stride = 0.6
lam_shrink = 0.3
eps_norm = 1e-06


def in_blocks(x, dim, count):
    lengths = x.shape
    blocks = x.reshape(*lengths[:dim], count, lengths[dim] // count, *lengths[dim + 1 :])
    return jnp.moveaxis(blocks, dim, 0)


def sum_at_owner(x, axis, dim):
    blocks = in_blocks(x, dim, lax.axis_size(axis))
    arrived = lax.all_to_all(blocks, axis, split_axis=0, concat_axis=0, tiled=True)
    return arrived.sum(axis=0)


def in_order(blocks, dim):
    blocks = jnp.moveaxis(blocks, 0, dim)
    lengths = blocks.shape
    return blocks.reshape(*lengths[:dim], lengths[dim] * lengths[dim + 1], *lengths[dim + 2 :])


def from_everyone(x, axis):
    copies = jnp.broadcast_to(x, (lax.axis_size(axis), *x.shape))
    return lax.all_to_all(copies, axis, split_axis=0, concat_axis=0, tiled=True)


def collect(x, axis, dim):
    return in_order(from_everyone(x, axis), dim)


def over_copies(x, axis):
    return from_everyone(x, axis).sum(axis=0)


def project_rows(rounded_amount, columns):
    return lax.dot_general(
        rounded_amount, columns, (((1,), (1,)), ((), ())), preferred_element_type=jnp.float32
    )


def residual_of(sampled_correlations, partial_value):
    shares = sum_at_owner(partial_value, "pix", 1)
    width = shares.shape[1]
    own_rows = lax.dynamic_slice_in_dim(
        sampled_correlations, lax.axis_index("pix") * width, width, 1
    )
    return collect((own_rows - shares).astype(jnp.bfloat16), "pix", 1)


def on_device(sensing_operator_parts, sampled_correlations, first_sky_estimate, patch_order_record):
    sensing_operator = sensing_operator_parts[0]
    chans, m_dev = sampled_correlations.shape
    share_width = first_sky_estimate.shape[3]
    tiles_share = share_width // TILE
    keep_count = tiles_share * lax.axis_size("base") * lax.axis_size("pix") // 4
    base_index = lax.axis_index("base")
    own_share = first_sky_estimate[:, 0, 0, :]
    current = own_share
    for step in range(ITERS):
        rounded_amount = current.astype(jnp.bfloat16)
        partial_value = project_rows(collect(rounded_amount, "base", 1), sensing_operator)
        resid = residual_of(sampled_correlations, partial_value)
        gradient_portion = jnp.dot(resid, sensing_operator, preferred_element_type=jnp.float32)
        grad_share = sum_at_owner(gradient_portion, "base", 1)
        moved = current + descent_stride * grad_share
        tiles = moved.reshape(chans, tiles_share, TILE)
        local_sum = jnp.sum(tiles * tiles, axis=(0, 2))
        total = over_copies(local_sum, "freq")
        ranks = lax.dynamic_slice_in_dim(
            patch_order_record[step], base_index * tiles_share, tiles_share, 0
        )
        rms_tile = jnp.sqrt(total / (CH * TILE) + eps_norm)
        keeping = (ranks < keep_count).astype(jnp.float32)
        factor = keeping * rms_tile / (rms_tile + lam_shrink)
        current = (tiles * factor[None, :, None]).reshape(chans, share_width)
    return current.reshape(chans, 1, 1, share_width)


def solution(mesh):
    in_specs = (
        P("freq", "base", "pix"),
        P("freq", "base"),
        P("freq", "pix", "base", None),
        P(None, "pix"),
    )
    out_specs = P("freq", "pix", "base", None)
    return jax.shard_map(
        on_device, mesh=mesh, in_specs=in_specs, out_specs=out_specs, check_vma=False
    )
```

profile of v0, /device:TPU:8, one launch (start us, length us, event | category | flops | bytes accessed | tf_op | source)
XLA Modules:
  0.0 440.1 jit_solution(8745866736782644324)
XLA Ops:
  0.0 0.8 convert_element_type.42
  0.8 16.4 %all_to_all.156 = bf16[16,32,128]{2,1,0:T(8,128)(2,1)S(1)} all-to-all(bf16[16,32,128]{2,1,0:T(8,128)(2,1)S(1)} %broadcast_in_dim.60), channel_id=1, replica_groups=mesh['freq'=2,'base'=16,'pix'=16] {'base'}, dimensions={0} | all-to-all | bytes 262144 | tf_op jit(solution)/shard_map/all_to_all | solution.py:36
  17.3 4.2 convolution_bitcast_fusion.5
  21.5 0.8 reshape.511
  22.3 10.4 %all-to-all-start.1 = ((f32[16,1,2048]{2,1,0:T(1,128)}), f32[16,1,2048]{2,1,0:T(1,128)S(1)}, u32[]{:S(2)}, u32[]{:S(2)}) async-start(f32[16,1,2048]{2,1,0:T(1,128)} %reshape.511), calls=%async_computation.1 | async-start | bytes 262144 | tf_op jit(solution)/shard_map/all_to_all | solution.py:24
  32.8 8.6 %all-to-all-done.1 = f32[16,1,2048]{2,1,0:T(1,128)S(1)} async-done(((f32[16,1,2048]{2,1,0:T(1,128)}), f32[16,1,2048]{2,1,0:T(1,128)S(1)}, u32[]{:S(2)}, u32[]{:S(2)}) %all-to-all-start.1) | async-done | bytes 131104 | tf_op jit(solution)/shard_map/all_to_all | solution.py:24
  41.9 0.9 reduce.18
  43.1 0.8 reshape.513
  43.8 3.5 all-to-all-start.2
  47.4 6.4 %copy.79 = bf16[2048,1024]{1,0:T(8,128)(2,1)} copy(bf16[2048,1024]{0,1:T(8,128)(2,1)} %bitcast.149) | data formatting | bytes 8388608 | tf_op jit(solution)/shard_map/dot_general | solution.py:75
  53.8 1.3 all-to-all-done.2
  55.4 4.2 convolution_bitcast_fusion.11
  59.7 3.9 all-to-all-start.3
  63.6 0.7 fusion.14
  64.3 10.1 %all-to-all-done.3 = f32[16,32,128]{2,1,0:T(8,128)S(1)} async-done(((f32[16,32,128]{2,1,0:T(8,128)}), f32[16,32,128]{2,1,0:T(8,128)S(1)}, u32[]{:S(2)}, u32[]{:S(2)}) %all-to-all-start.3) | async-done | bytes 262176 | tf_op jit(solution)/shard_map/all_to_all | solution.py:24
  75.6 9.1 %all_to_all.157 = f32[2,1,1]{2,1,0:T(1,128)S(1)} all-to-all(f32[2,1,1]{2,1,0:T(1,128)S(1)} %broadcast_in_dim.62), channel_id=1, replica_groups=mesh['freq'=2,'base'=16,'pix'=16] {'freq'}, dimensions={0} | all-to-all | bytes 16 | tf_op jit(solution)/shard_map/all_to_all | solution.py:36
  86.7 12.2 %all_to_all.158 = bf16[16,32,128]{2,1,0:T(8,128)(2,1)S(1)} all-to-all(bf16[16,32,128]{2,1,0:T(8,128)(2,1)S(1)} %broadcast_in_dim.63), channel_id=1, replica_groups=mesh['freq'=2,'base'=16,'pix'=16] {'base'}, dimensions={0} | all-to-all | bytes 262144 | tf_op jit(solution)/shard_map/all_to_all | solution.py:36
  99.1 4.2 convolution_bitcast_fusion.4
  103.5 14.1 %all_to_all.159 = f32[16,1,2048]{2,1,0:T(1,128)S(1)} all-to-all(f32[16,1,2048]{2,1,0:T(1,128)S(1)} %reshape.515), channel_id=1, replica_groups=mesh['freq'=2,'base'=16,'pix'=16] {'pix'}, dimensions={0} | all-to-all | bytes 262144 | tf_op jit(solution)/shard_map/all_to_all | solution.py:24
  117.7 0.9 reduce.19
  118.9 10.7 %all_to_all.160 = bf16[16,2,1024]{2,1,0:T(2,128)(2,1)S(1)} all-to-all(bf16[16,2,1024]{2,1,0:T(2,128)(2,1)S(1)} %reshape.517), channel_id=1, replica_groups=mesh['freq'=2,'base'=16,'pix'=16] {'pix'}, dimensions={0} | all-to-all | bytes 131072 | tf_op jit(solution)/shard_map/all_to_all | solution.py:36
  130.0 3.5 convolution_bitcast_fusion.10
  133.5 14.3 %all_to_all.161 = f32[16,32,128]{2,1,0:T(8,128)S(1)} all-to-all(f32[16,32,128]{2,1,0:T(8,128)S(1)} %convolution_bitcast_fusion.10), channel_id=1, replica_groups=mesh['freq'=2,'base'=16,'pix'=16] {'base'}, dimensions={0} | all-to-all | bytes 524288 | tf_op jit(solution)/shard_map/all_to_all | solution.py:24
  149.1 7.6 %all_to_all.162 = f32[2,1,1]{2,1,0:T(1,128)S(1)} all-to-all(f32[2,1,1]{2,1,0:T(1,128)S(1)} %broadcast_in_dim.65), channel_id=1, replica_groups=mesh['freq'=2,'base'=16,'pix'=16] {'freq'}, dimensions={0} | all-to-all | bytes 16 | tf_op jit(solution)/shard_map/all_to_all | solution.py:36
  158.7 12.2 %all_to_all.163 = bf16[16,32,128]{2,1,0:T(8,128)(2,1)S(1)} all-to-all(bf16[16,32,128]{2,1,0:T(8,128)(2,1)S(1)} %broadcast_in_dim.66), channel_id=1, replica_groups=mesh['freq'=2,'base'=16,'pix'=16] {'base'}, dimensions={0} | all-to-all | bytes 262144 | tf_op jit(solution)/shard_map/all_to_all | solution.py:36
  171.0 4.2 convolution_bitcast_fusion.3
  175.5 11.2 %all_to_all.164 = f32[16,1,2048]{2,1,0:T(1,128)S(1)} all-to-all(f32[16,1,2048]{2,1,0:T(1,128)S(1)} %reshape.519), channel_id=1, replica_groups=mesh['freq'=2,'base'=16,'pix'=16] {'pix'}, dimensions={0} | all-to-all | bytes 262144 | tf_op jit(solution)/shard_map/all_to_all | solution.py:24
  186.7 0.9 reduce.20
  188.0 10.8 %all_to_all.165 = bf16[16,2,1024]{2,1,0:T(2,128)(2,1)S(1)} all-to-all(bf16[16,2,1024]{2,1,0:T(2,128)(2,1)S(1)} %reshape.521), channel_id=1, replica_groups=mesh['freq'=2,'base'=16,'pix'=16] {'pix'}, dimensions={0} | all-to-all | bytes 131072 | tf_op jit(solution)/shard_map/all_to_all | solution.py:36
  199.2 4.2 convolution_bitcast_fusion.9
  203.4 4.1 all-to-all-start.13
  208.1 10.3 %all-to-all-done.13 = f32[16,32,128]{2,1,0:T(8,128)S(1)} async-done(((f32[16,32,128]{2,1,0:T(8,128)}), f32[16,32,128]{2,1,0:T(8,128)S(1)}, u32[]{:S(2)}, u32[]{:S(2)}) %all-to-all-start.13) | async-done | bytes 262176 | tf_op jit(solution)/shard_map/all_to_all | solution.py:24
  219.6 7.6 %all_to_all.166 = f32[2,1,1]{2,1,0:T(1,128)S(1)} all-to-all(f32[2,1,1]{2,1,0:T(1,128)S(1)} %broadcast_in_dim.68), channel_id=1, replica_groups=mesh['freq'=2,'base'=16,'pix'=16] {'freq'}, dimensions={0} | all-to-all | bytes 16 | tf_op jit(solution)/shard_map/all_to_all | solution.py:36
  229.2 12.4 %all_to_all.167 = bf16[16,32,128]{2,1,0:T(8,128)(2,1)S(1)} all-to-all(bf16[16,32,128]{2,1,0:T(8,128)(2,1)S(1)} %broadcast_in_dim.69), channel_id=1, replica_groups=mesh['freq'=2,'base'=16,'pix'=16] {'base'}, dimensions={0} | all-to-all | bytes 262144 | tf_op jit(solution)/shard_map/all_to_all | solution.py:36
  241.8 4.2 convolution_bitcast_fusion.2
  246.2 11.2 %all_to_all.168 = f32[16,1,2048]{2,1,0:T(1,128)S(1)} all-to-all(f32[16,1,2048]{2,1,0:T(1,128)S(1)} %reshape.523), channel_id=1, replica_groups=mesh['freq'=2,'base'=16,'pix'=16] {'pix'}, dimensions={0} | all-to-all | bytes 262144 | tf_op jit(solution)/shard_map/all_to_all | solution.py:24
  257.5 0.9 reduce.21
  258.7 10.7 %all_to_all.169 = bf16[16,2,1024]{2,1,0:T(2,128)(2,1)S(1)} all-to-all(bf16[16,2,1024]{2,1,0:T(2,128)(2,1)S(1)} %reshape.525), channel_id=1, replica_groups=mesh['freq'=2,'base'=16,'pix'=16] {'pix'}, dimensions={0} | all-to-all | bytes 131072 | tf_op jit(solution)/shard_map/all_to_all | solution.py:36
  269.8 3.5 convolution_bitcast_fusion.8
  273.3 14.3 %all_to_all.170 = f32[16,32,128]{2,1,0:T(8,128)S(1)} all-to-all(f32[16,32,128]{2,1,0:T(8,128)S(1)} %convolution_bitcast_fusion.8), channel_id=1, replica_groups=mesh['freq'=2,'base'=16,'pix'=16] {'base'}, dimensions={0} | all-to-all | bytes 524288 | tf_op jit(solution)/shard_map/all_to_all | solution.py:24
  287.6 0.6 multiply_reduce_fusion.1
  288.8 7.6 %all_to_all.171 = f32[2,1,1]{2,1,0:T(1,128)S(1)} all-to-all(f32[2,1,1]{2,1,0:T(1,128)S(1)} %broadcast_in_dim.71), channel_id=1, replica_groups=mesh['freq'=2,'base'=16,'pix'=16] {'freq'}, dimensions={0} | all-to-all | bytes 16 | tf_op jit(solution)/shard_map/all_to_all | solution.py:36
  298.5 12.2 %all_to_all.172 = bf16[16,32,128]{2,1,0:T(8,128)(2,1)S(1)} all-to-all(bf16[16,32,128]{2,1,0:T(8,128)(2,1)S(1)} %broadcast_in_dim.72), channel_id=1, replica_groups=mesh['freq'=2,'base'=16,'pix'=16] {'base'}, dimensions={0} | all-to-all | bytes 262144 | tf_op jit(solution)/shard_map/all_to_all | solution.py:36
  310.8 4.2 convolution_bitcast_fusion.1
  315.2 11.2 %all_to_all.173 = f32[16,1,2048]{2,1,0:T(1,128)S(1)} all-to-all(f32[16,1,2048]{2,1,0:T(1,128)S(1)} %reshape.527), channel_id=1, replica_groups=mesh['freq'=2,'base'=16,'pix'=16] {'pix'}, dimensions={0} | all-to-all | bytes 262144 | tf_op jit(solution)/shard_map/all_to_all | solution.py:24
  326.5 0.9 reduce.22
  327.7 10.7 %all_to_all.174 = bf16[16,2,1024]{2,1,0:T(2,128)(2,1)S(1)} all-to-all(bf16[16,2,1024]{2,1,0:T(2,128)(2,1)S(1)} %reshape.529), channel_id=1, replica_groups=mesh['freq'=2,'base'=16,'pix'=16] {'pix'}, dimensions={0} | all-to-all | bytes 131072 | tf_op jit(solution)/shard_map/all_to_all | solution.py:36
  338.7 4.2 convolution_bitcast_fusion.7
  343.0 4.1 all-to-all-start.23
  347.0 0.7 fusion.16
  347.7 10.3 %all-to-all-done.23 = f32[16,32,128]{2,1,0:T(8,128)S(1)} async-done(((f32[16,32,128]{2,1,0:T(8,128)}), f32[16,32,128]{2,1,0:T(8,128)S(1)}, u32[]{:S(2)}, u32[]{:S(2)}) %all-to-all-start.23) | async-done | bytes 262176 | tf_op jit(solution)/shard_map/all_to_all | solution.py:24
  359.2 7.6 %all_to_all.175 = f32[2,1,1]{2,1,0:T(1,128)S(1)} all-to-all(f32[2,1,1]{2,1,0:T(1,128)S(1)} %broadcast_in_dim.74), channel_id=1, replica_groups=mesh['freq'=2,'base'=16,'pix'=16] {'freq'}, dimensions={0} | all-to-all | bytes 16 | tf_op jit(solution)/shard_map/all_to_all | solution.py:36
  368.8 12.4 %all_to_all.176 = bf16[16,32,128]{2,1,0:T(8,128)(2,1)S(1)} all-to-all(bf16[16,32,128]{2,1,0:T(8,128)(2,1)S(1)} %broadcast_in_dim.75), channel_id=1, replica_groups=mesh['freq'=2,'base'=16,'pix'=16] {'base'}, dimensions={0} | all-to-all | bytes 262144 | tf_op jit(solution)/shard_map/all_to_all | solution.py:36
  381.4 4.2 convolution_bitcast_fusion
  385.8 11.2 %all_to_all.177 = f32[16,1,2048]{2,1,0:T(1,128)S(1)} all-to-all(f32[16,1,2048]{2,1,0:T(1,128)S(1)} %reshape.531), channel_id=1, replica_groups=mesh['freq'=2,'base'=16,'pix'=16] {'pix'}, dimensions={0} | all-to-all | bytes 262144 | tf_op jit(solution)/shard_map/all_to_all | solution.py:24
  397.1 0.9 reduce.23
  398.3 10.7 %all_to_all.178 = bf16[16,2,1024]{2,1,0:T(2,128)(2,1)S(1)} all-to-all(bf16[16,2,1024]{2,1,0:T(2,128)(2,1)S(1)} %reshape.533), channel_id=1, replica_groups=mesh['freq'=2,'base'=16,'pix'=16] {'pix'}, dimensions={0} | all-to-all | bytes 131072 | tf_op jit(solution)/shard_map/all_to_all | solution.py:36
  409.3 4.2 convolution_bitcast_fusion.6
  413.6 4.0 all-to-all-start.28
  417.6 10.9 %all-to-all-done.28 = f32[16,32,128]{2,1,0:T(8,128)S(1)} async-done(((f32[16,32,128]{2,1,0:T(8,128)}), f32[16,32,128]{2,1,0:T(8,128)S(1)}, u32[]{:S(2)}, u32[]{:S(2)}) %all-to-all-start.28) | async-done | bytes 262176 | tf_op jit(solution)/shard_map/all_to_all | solution.py:24
  428.5 0.7 fusion.1
  429.2 0.7 broadcast_in_dim.77
  429.9 7.6 %all_to_all.179 = f32[2,1,1]{2,1,0:T(1,128)S(1)} all-to-all(f32[2,1,1]{2,1,0:T(1,128)S(1)} %broadcast_in_dim.77), channel_id=1, replica_groups=mesh['freq'=2,'base'=16,'pix'=16] {'freq'}, dimensions={0} | all-to-all | bytes 16 | tf_op jit(solution)/shard_map/all_to_all | solution.py:36
  439.5 0.6 add_multiply_fusion
  (107 shorter events, 16.4 us)
Async XLA Ops:
  0.0 43.0 %copy-start.1 = (f32[32,1024]{1,0:T(8,128)S(1)}, f32[32,1024]{1,0:T(8,128)}, u32[]{:S(2)}) copy-start(f32[32,1024]{1,0:T(8,128)} %param.5) | copy-start | bytes 393220
  22.3 19.1 %all-to-all-start.1 = ((f32[16,1,2048]{2,1,0:T(1,128)}), f32[16,1,2048]{2,1,0:T(1,128)S(1)}, u32[]{:S(2)}, u32[]{:S(2)}) async-start(f32[16,1,2048]{2,1,0:T(1,128)} %reshape.511), calls=%async_computation.1 | async-start | bytes 262144 | tf_op jit(solution)/shard_map/all_to_all | solution.py:24
  43.8 11.2 %all-to-all-start.2 = ((bf16[16,2,1024]{2,1,0:T(2,128)(2,1)}), bf16[16,2,1024]{2,1,0:T(2,128)(2,1)S(1)}, u32[]{:S(2)}, u32[]{:S(2)}) async-start(bf16[16,2,1024]{2,1,0:T(2,128)(2,1)} %reshape.513), calls=%async_computation.2 | async-start | bytes 131072 | tf_op jit(solution)/shard_map/all_to_all | solution.py:36
  53.8 9.8 %copy-start.2 = (s32[6,16]{1,0:T(8,128)S(1)}, s32[6,16]{1,0:T(8,128)}, u32[]{:S(2)}) copy-start(s32[6,16]{1,0:T(8,128)} %param.7) | copy-start | bytes 1156
  53.8 20.6 %copy-start = (f32[32,1,1,128]{3,2,1,0:T(1,128)S(1)}, f32[32,1,1,128]{3,2,1,0:T(1,128)}, u32[]{:S(2)}) copy-start(f32[32,1,1,128]{3,2,1,0:T(1,128)} %param.6) | copy-start | bytes 49156
  59.7 14.7 %all-to-all-start.3 = ((f32[16,32,128]{2,1,0:T(8,128)}), f32[16,32,128]{2,1,0:T(8,128)S(1)}, u32[]{:S(2)}, u32[]{:S(2)}) async-start(f32[16,32,128]{2,1,0:T(8,128)} %convolution_bitcast_fusion.11), calls=%async_computation.3 | async-start | bytes 524288 | tf_op jit(solution)/shard_map/all_to_all | solution.py:24
  203.4 15.0 %all-to-all-start.13 = ((f32[16,32,128]{2,1,0:T(8,128)}), f32[16,32,128]{2,1,0:T(8,128)S(1)}, u32[]{:S(2)}, u32[]{:S(2)}) async-start(f32[16,32,128]{2,1,0:T(8,128)} %convolution_bitcast_fusion.9), calls=%async_computation.13 | async-start | bytes 524288 | tf_op jit(solution)/shard_map/all_to_all | solution.py:24
  343.0 15.0 %all-to-all-start.23 = ((f32[16,32,128]{2,1,0:T(8,128)}), f32[16,32,128]{2,1,0:T(8,128)S(1)}, u32[]{:S(2)}, u32[]{:S(2)}) async-start(f32[16,32,128]{2,1,0:T(8,128)} %convolution_bitcast_fusion.7), calls=%async_computation.23 | async-start | bytes 524288 | tf_op jit(solution)/shard_map/all_to_all | solution.py:24
  413.6 14.9 %all-to-all-start.28 = ((f32[16,32,128]{2,1,0:T(8,128)}), f32[16,32,128]{2,1,0:T(8,128)S(1)}, u32[]{:S(2)}, u32[]{:S(2)}) async-start(f32[16,32,128]{2,1,0:T(8,128)} %convolution_bitcast_fusion.6), calls=%async_computation.28 | async-start | bytes 524288 | tf_op jit(solution)/shard_map/all_to_all | solution.py:24
where the time goes:
time: 442 us; the launch traced here: 440 us
  blocking collectives  266 us (60%)
  waiting for transfers between devices  51.5 us (12%)
  matrix products  49.2 us (11%)
  starting transfers between devices  30 us (7%)
  local copies, waits for them, and re-layouts  17.5 us (4%)
  other arithmetic  16.9 us (4%)
  between operations  8.72 us (2%)
    all_to_all x17, blocking collectives, from_everyone(): return lax.all_to_all(copies, axis, split_axis=0, concat_axis=0, tiled=True)  179 us
    all_to_all x7, blocking collectives, sum_at_owner(): lax.all_to_all(blocks, axis, split_axis=0, concat_axis=0, tiled=True)  87.7 us
    all_to_all x5, waiting for transfers between devices, sum_at_owner(): lax.all_to_all(blocks, axis, split_axis=0, concat_axis=0, tiled=True)  50.2 us
    all_to_all x5, starting transfers between devices, sum_at_owner(): lax.all_to_all(blocks, axis, split_axis=0, concat_axis=0, tiled=True)  26.5 us
    dot_general x6, matrix products, project_rows(): lax.dot_general(rounded_amount, columns, (((1,), (1,)), ((), ())), prefer...  25.3 us
    dot_general x6, matrix products, on_device(): jnp.dot(resid, sensing_operator, preferred_element_type=jnp.float32)  23.9 us
  transfers between devices with their start and end apart: 6, of which 6 were waited for; matrix products, arithmetic and copies ran while one was open for 2% of the time, Pallas kernels for 0%

commit v1 on v0

v1 whole, which is shorter than its diff:
```python
import functools

import jax
import jax.numpy as jnp
from jax import lax
from jax.experimental import pallas as pl
from jax.experimental.pallas import tpu as pltpu
from jax.sharding import PartitionSpec as P

CH = 64
TILE = 128
ITERS = 6
STRIDE = 0.6
SHRINK = 0.3
EPS = 1e-06

F32 = jnp.float32
BF16 = jnp.bfloat16


def outward(n):
    out = [n // 2] if n > 1 else []
    for d in range((n - 1) // 2, 0, -1):
        out += [d, n - d]
    return out + [0]


def local_wait(ref, sem):
    pltpu.make_async_copy(ref, ref, sem).wait()


def kernel(
    nb, npx, keep_count,
    a_hbm, y_hbm, x0_hbm, rank_ref, out_ref,
    a_s, y_s, z_s, keep_s,
    zst, zrv, nst, nrv, acc, pst, prv, rst, rrv, gacc, gst, grv,
    in_sem, zs, zr, ns, nr, ps, pr, rs, rr, gs, gr,
):
    ny, nz = nb // 2, npx // 2
    f, b, p = lax.axis_index("freq"), lax.axis_index("base"), lax.axis_index("pix")
    xl, yy = b // ny, b % ny
    zz, cc = p // 2, p % 2
    rows = nz * TILE

    copy_x0 = pltpu.make_async_copy(x0_hbm, z_s, in_sem.at[0])
    copy_a = pltpu.make_async_copy(a_hbm, a_s, in_sem.at[1])
    copy_y = pltpu.make_async_copy(y_hbm, y_s, in_sem.at[2])
    copy_x0.start()
    copy_a.start()
    copy_y.start()

    base_peers = [((xl + dx) % 2 * ny + (yy + dy) % ny) for dy in outward(ny) for dx in (1, 0)]
    pix_peers = [((zz + dz) % nz, (cc + dc) % 2) for dz in outward(nz) for dc in (1, 0)]

    barrier = pltpu.get_barrier_semaphore()
    for other in base_peers:
        pl.semaphore_signal(barrier, 1, device_id={"freq": 1 - f, "base": other}, device_id_type=pl.DeviceIdType.MESH)
    for other in base_peers[:-1]:
        pl.semaphore_signal(barrier, 1, device_id={"base": other}, device_id_type=pl.DeviceIdType.MESH)
    for oz, oc in pix_peers[:-1]:
        pl.semaphore_signal(barrier, 1, device_id={"pix": oz * 2 + oc}, device_id_type=pl.DeviceIdType.MESH)

    same = lax.broadcasted_iota(jnp.int32, (nb, nb), 0) == lax.broadcasted_iota(jnp.int32, (nb, nb), 1)
    for k in range(ITERS):
        row = jnp.broadcast_to(rank_ref[k : k + 1, :], (nb, nb))
        column = jnp.sum(jnp.where(same & (row < keep_count), 1.0, 0.0), axis=1, keepdims=True)
        keep_s[k] = jnp.broadcast_to(column, (nb, TILE)).reshape(nb, 1, TILE)

    copy_x0.wait()
    copy_y.wait()
    pl.semaphore_wait(barrier, 2 * nb - 1 + npx - 1)
    copy_a.wait()

    def remote(src, dst, send, recv, where):
        return pltpu.make_async_remote_copy(
            src_ref=src, dst_ref=dst, send_sem=send, recv_sem=recv,
            device_id=where, device_id_type=pl.DeviceIdType.MESH,
        )

    def factor(k, tile):
        par = k % 2
        total = jnp.sum(nrv[par, 0, tile] + nrv[par, 1, tile], axis=1, keepdims=True)
        rms = jnp.sqrt(total / (CH * TILE) + EPS)
        value = keep_s[(k + ITERS - 1) % ITERS, tile] * (rms / (rms + SHRINK))
        return jnp.where(k == 0, 1.0, value)

    def norm_copies(k, to_all):
        par = k % 2
        out = []
        for i, other in enumerate(base_peers if to_all else [b]):
            out.append(remote(nst, nrv.at[par, f, b], ns.at[1, i], nr.at[par, f, b], {"freq": 1 - f, "base": other}))
        if to_all:
            for i, other in enumerate(base_peers[:-1]):
                out.append(remote(nst, nrv.at[par, f, b], ns.at[0, i], nr.at[par, f, b], {"base": other}))
        return out

    def put_norm(k, z):
        par = k % 2
        nst[...] = jnp.sum(z * z, axis=0, keepdims=True)
        return pltpu.make_async_copy(nst, nrv.at[par, f, b], nr.at[par, f, b])

    def step(k, carry):
        par = k % 2
        z = z_s[...]
        zst[...] = z.astype(BF16)
        own_norm = put_norm(k, z)
        own_z = pltpu.make_async_copy(zst, zrv.at[b], zr.at[b])
        n_sends = norm_copies(k, True)
        z_sends = [
            remote(zst, zrv.at[b], zs.at[i], zr.at[b], {"base": other})
            for i, other in enumerate(base_peers[:-1])
        ]
        own_z.start()
        own_norm.start()
        for c in n_sends:
            c.start()
        for c in z_sends:
            c.start()

        nq = ny // 2
        for i, dq in enumerate(reversed(outward(nq))):
            for dx in (0, 1):
                t0 = (xl + dx) % 2 * ny + (yy // 2 + dq) % nq * 2
                parts = []
                for t in (t0, t0 + 1):
                    local_wait(zrv.at[t], zr.at[t])
                    local_wait(nrv.at[par, 0, t], nr.at[par, 0, t])
                    local_wait(nrv.at[par, 1, t], nr.at[par, 1, t])
                    parts.append((zrv[t].astype(F32) * factor(k, t)).astype(BF16))
                lhs = jnp.concatenate(parts, axis=1)
                columns = pl.ds(pl.multiple_of(t0 * TILE, 2 * TILE), 2 * TILE)
                for n in range(0, rows, 256):
                    part = lax.dot_general(
                        lhs, a_s[n : n + 256, columns], (((1,), (1,)), ((), ())), preferred_element_type=F32
                    )
                    if i == 0 and dx == 0:
                        acc[:, n : n + 256] = part
                    else:
                        acc[:, n : n + 256] += part

        for z_ in range(nz):
            for c_ in range(2):
                pst[z_, c_] = acc[16 * c_ : 16 * c_ + 16, TILE * z_ : TILE * z_ + TILE].astype(BF16)
        p_sends = [
            remote(pst.at[oz, oc], prv.at[zz, cc], ps.at[i], pr.at[zz, cc], {"pix": oz * 2 + oc})
            for i, (oz, oc) in enumerate(pix_peers[:-1])
        ]
        for c in p_sends:
            c.start()
        total = pst[zz, cc].astype(F32)
        for oz, oc in reversed(pix_peers[:-1]):
            local_wait(prv.at[oz, oc], pr.at[oz, oc])
            total += prv[oz, oc].astype(F32)
        own_y = y_s[pl.ds(pl.multiple_of(cc * 16, 16), 16), pl.ds(pl.multiple_of(zz * TILE, TILE), TILE)]
        rst[...] = (own_y - total).astype(BF16)

        own_r = pltpu.make_async_copy(rst, rrv.at[zz, cc], rr.at[zz, cc])
        r_sends = [
            remote(rst, rrv.at[zz, cc], rs.at[i], rr.at[zz, cc], {"pix": oz * 2 + oc})
            for i, (oz, oc) in enumerate(pix_peers[:-1])
        ]
        own_r.start()
        for c in r_sends:
            c.start()
        nq = nz // 2
        for i, dq in enumerate(reversed(outward(nq))):
            z0 = (zz // 2 + dq) % nq * 2
            parts = []
            for z_ in (z0, z0 + 1):
                local_wait(rrv.at[z_, 0], rr.at[z_, 0])
                local_wait(rrv.at[z_, 1], rr.at[z_, 1])
                parts.append(jnp.concatenate([rrv[z_, 0], rrv[z_, 1]], axis=0))
            lhs = jnp.concatenate(parts, axis=1)
            these = pl.ds(pl.multiple_of(z0 * TILE, 2 * TILE), 2 * TILE)
            for n in range(nb // 2):
                part = jnp.dot(lhs, a_s[these, n * 256 : n * 256 + 256], preferred_element_type=F32)
                if i == 0:
                    gacc[n] = part
                else:
                    gacc[n] += part

        g_sends = [
            remote(gst.at[other], grv.at[b], gs.at[i], gr.at[b], {"base": other})
            for i, other in enumerate(base_peers[:-1])
        ]

        @pl.when(k > 0)
        def _():
            for c in g_sends:
                c.wait_send()

        for n in range(nb // 2):
            gst[2 * n] = gacc[n, :, :TILE].astype(BF16)
            gst[2 * n + 1] = gacc[n, :, TILE:].astype(BF16)
        for c in g_sends:
            c.start()
        for c in n_sends + z_sends + p_sends + r_sends:
            c.wait_send()
        x = z_s[...] * factor(k, b)
        total = gst[b].astype(F32)
        for other in reversed(base_peers[:-1]):
            local_wait(grv.at[other], gr.at[other])
            total += grv[other].astype(F32)
        z_s[...] = x + STRIDE * total
        return carry

    lax.fori_loop(0, ITERS, step, 0)

    for i, other in enumerate(base_peers[:-1]):
        remote(gst.at[other], grv.at[b], gs.at[i], gr.at[b], {"base": other}).wait_send()
    z = z_s[...]
    own_norm = put_norm(ITERS, z)
    (send,) = norm_copies(ITERS, False)
    send.start()
    own_norm.start()
    par = ITERS % 2
    for g in range(2):
        local_wait(nrv.at[par, g, b], nr.at[par, g, b])
    send.wait_send()
    out_ref[...] = z * factor(ITERS, b)


def on_device(nb, npx, sensing_operator_parts, sampled_correlations, first_sky_estimate, patch_order_record):
    a = sensing_operator_parts[0]
    chans, rows = sampled_correlations.shape
    pixels = a.shape[1]
    nz = npx // 2
    dma = pltpu.SemaphoreType.DMA
    anywhere = pl.BlockSpec(memory_space=pl.ANY)
    vmem = pl.BlockSpec(memory_space=pltpu.VMEM)
    image = pl.pallas_call(
        functools.partial(kernel, nb, npx, nb * npx // 4),
        out_shape=jax.ShapeDtypeStruct((chans, TILE), F32),
        in_specs=[anywhere, anywhere, anywhere, vmem],
        out_specs=vmem,
        scratch_shapes=[
            pltpu.VMEM((rows, pixels), BF16),
            pltpu.VMEM((chans, rows), F32),
            pltpu.VMEM((chans, TILE), F32),
            pltpu.VMEM((ITERS, nb, 1, TILE), F32),
            pltpu.VMEM((chans, TILE), BF16),
            pltpu.VMEM((nb, chans, TILE), BF16),
            pltpu.VMEM((1, TILE), F32),
            pltpu.VMEM((2, 2, nb, 1, TILE), F32),
            pltpu.VMEM((chans, rows), F32),
            pltpu.VMEM((nz, 2, 16, TILE), BF16),
            pltpu.VMEM((nz, 2, 16, TILE), BF16),
            pltpu.VMEM((16, TILE), BF16),
            pltpu.VMEM((nz, 2, 16, TILE), BF16),
            pltpu.VMEM((nb // 2, chans, 2 * TILE), F32),
            pltpu.VMEM((nb, chans, TILE), BF16),
            pltpu.VMEM((nb, chans, TILE), BF16),
            dma((3,)),
            dma((nb,)), dma((nb,)),
            dma((2, nb)), dma((2, 2, nb)),
            dma((npx,)), dma((nz, 2)),
            dma((npx,)), dma((nz, 2)),
            dma((nb,)), dma((nb,)),
        ],
        compiler_params=pltpu.CompilerParams(collective_id=0, has_side_effects=True),
        name="shrinkage",
    )(a, sampled_correlations, first_sky_estimate.reshape(chans, TILE), patch_order_record)
    return image.reshape(chans, 1, 1, TILE)


def solution(mesh):
    in_specs = (
        P("freq", "base", "pix"),
        P("freq", "base"),
        P("freq", "pix", "base", None),
        P(None, "pix"),
    )
    out_specs = P("freq", "pix", "base", None)
    return jax.shard_map(
        functools.partial(on_device, mesh.shape["base"], mesh.shape["pix"]),
        mesh=mesh, in_specs=in_specs, out_specs=out_specs, check_vma=False,
    )
```

time: 442 us -> 160 us (0.36)
  blocking collectives: 266 us -> 0 us
  Pallas kernels: 0 us -> 158 us
  waiting for transfers between devices: 51.5 us -> 0 us
  matrix products: 49.2 us -> 0 us
  starting transfers between devices: 30 us -> 0 us
  other arithmetic: 16.9 us -> 0 us
  local copies, waits for them, and re-layouts: 17.5 us -> 1.32 us
  between operations: 8.72 us -> 0.01 us
    all_to_all x24 -> x0, blocking collectives: 266 us -> none  [the longest x17 179 us: from_everyone(): return lax.all_to_all(copies, axis, split_axis=0, concat_axis=0, tiled=True)]
    pallas_call x0 -> x1, Pallas kernels: none -> 158 us  [on_device(): pl.pallas_call(functools.partial(kernel, nb, npx, nb * npx // 4), out_sha...]
    all_to_all x6 -> x0, waiting for transfers between devices: 51.5 us -> none  [the longest x5 50.2 us: sum_at_owner(): lax.all_to_all(blocks, axis, split_axis=0, concat_axis=0, tiled=True)]
    dot_general x12 -> x0, matrix products: 49.2 us -> none  [the longest x6 25.3 us: project_rows(): lax.dot_general(rounded_amount, columns, (((1,), (1,)), ((), ())), prefer...]
    all_to_all x6 -> x0, starting transfers between devices: 30 us -> none  [the longest x5 26.5 us: sum_at_owner(): lax.all_to_all(blocks, axis, split_axis=0, concat_axis=0, tiled=True)]
    reduce_sum x24 -> x0, other arithmetic: 7.73 us -> none  [the longest x6 3.76 us: on_device(): local_sum = jnp.sum(tiles * tiles, axis=(0, 2))]
    dot_general x1 -> x0, local copies, waits for them, and re-layouts: 6.41 us -> none  [on_device(): jnp.dot(resid, sensing_operator, preferred_element_type=jnp.float32)]
    all_to_all x6 -> x0, other arithmetic: 5.26 us -> none  [sum_at_owner(): lax.all_to_all(blocks, axis, split_axis=0, concat_axis=0, tiled=True)]
  transfers between devices with their start and end apart: 6 -> 0, of which waited for: 6 -> 0; matrix products, arithmetic and copies ran while one was open for 2% -> 0% of each run, Pallas kernels for 0% -> 0%
where the time goes in v1:
time: 160 us; the launch traced here: 159 us
  Pallas kernels  158 us (99%)
    pallas_call x1, Pallas kernels, on_device(): pl.pallas_call(functools.partial(kernel, nb, npx, nb * npx // 4), out_sha...  158 us

profile of v1, /device:TPU:8, one launch (start us, length us, event | category | flops | bytes accessed | tf_op | source)
XLA Modules:
  0.0 159.5 jit_solution(5495941144867455446)
XLA Ops:
  0.0 158.1 %shrinkage.1 = f32[32,128]{1,0:T(8,128)} custom-call(bf16[1024,2048]{1,0:T(8,128)(2,1)} %bitcast.5, f32[32,1024]{1,0:T(8,128)} %y_hbm.1, f32[32,128]{1,0:T(8,128)} %bitcast.7, s32[6,16]{1,0:T(8,128)} %rank_ref.1), custom_call_target="tpu_custom_call" | custom-call | tf_op jit(solution)/shard_map/shrinkage/pallas_call | solution.py:231
  158.1 1.3 copy.7

commit v2 on v1

v2 whole, which is shorter than its diff:
```python
import functools

import jax
import jax.numpy as jnp
from jax import lax
from jax.experimental import pallas as pl
from jax.experimental.pallas import tpu as pltpu
from jax.sharding import PartitionSpec as P

CH = 64
TILE = 128
ITERS = 6
STRIDE = 0.6
SHRINK = 0.3
EPS = 1e-06
OWNER = 1

F32 = jnp.float32
BF16 = jnp.bfloat16


def outward(n):
    out = [n // 2] if n > 1 else []
    for d in range((n - 1) // 2, 0, -1):
        out += [d, n - d]
    return out + [0]


def local_wait(ref, sem):
    pltpu.make_async_copy(ref, ref, sem).wait()


def kernel(
    nb, npx, keep_count,
    a_hbm, y_hbm, x0_hbm, rank_ref, out_ref,
    a_s, at_s, y_s, z_s, keep_s,
    zrv, nst, nrv, acc, pst, prv, rrv, gacc, gst, grv,
    in_sem, zs, zr, ns, nr, ps, pr, rs, rr, gs, gr,
):
    ny, nz = nb // 2, npx // 2
    nq_y = ny // 2
    f, b, p = lax.axis_index("freq"), lax.axis_index("base"), lax.axis_index("pix")
    xl, yy = b // ny, b % ny
    zz, cc = p // 2, p % 2
    rows = nz * TILE

    copy_x0 = pltpu.make_async_copy(x0_hbm, z_s, in_sem.at[0])
    copy_a = pltpu.make_async_copy(a_hbm, a_s, in_sem.at[1])
    copy_y = pltpu.make_async_copy(y_hbm, y_s, in_sem.at[2])
    copy_x0.start()
    copy_a.start()
    copy_y.start()

    base_peers = [((xl + dx) % 2 * ny + (yy + dy) % ny) for dy in outward(ny) for dx in (1, 0)]
    pix_peers = [((zz + dz) % nz, (cc + dc) % 2) for dz in outward(nz) for dc in (1, 0)]

    barrier = pltpu.get_barrier_semaphore()
    for other in base_peers:
        pl.semaphore_signal(barrier, 1, device_id={"freq": 1 - f, "base": other}, device_id_type=pl.DeviceIdType.MESH)
    for other in base_peers[:-1]:
        pl.semaphore_signal(barrier, 1, device_id={"base": other}, device_id_type=pl.DeviceIdType.MESH)
    for oz, oc in pix_peers[:-1]:
        pl.semaphore_signal(barrier, 1, device_id={"pix": oz * 2 + oc}, device_id_type=pl.DeviceIdType.MESH)

    same = lax.broadcasted_iota(jnp.int32, (nb, nb), 0) == lax.broadcasted_iota(jnp.int32, (nb, nb), 1)
    for k in range(ITERS):
        row = jnp.broadcast_to(rank_ref[k : k + 1, :], (nb, nb))
        column = jnp.sum(jnp.where(same & (row < keep_count), 1.0, 0.0), axis=1, keepdims=True)
        keep_s[k] = jnp.broadcast_to(column, (nb, TILE)).reshape(nb, 1, TILE)

    copy_x0.wait()
    copy_y.wait()
    pl.semaphore_wait(barrier, 2 * nb - 1 + npx - 1)

    def remote(src, dst, send, recv, where):
        return pltpu.make_async_remote_copy(
            src_ref=src, dst_ref=dst, send_sem=send, recv_sem=recv,
            device_id=where, device_id_type=pl.DeviceIdType.MESH,
        )

    def norm_of(z):
        return jnp.sum(z * z, axis=0, keepdims=True)

    def factor(k, tile, own_norm):
        total = jnp.sum(own_norm + nrv[k % 2, tile], axis=1, keepdims=True)
        rms = jnp.sqrt(total / (CH * TILE) + EPS)
        value = keep_s[(k + ITERS - 1) % ITERS, tile] * (rms / (rms + SHRINK))
        return jnp.where(k == 0, 1.0, value)

    def norm_copies(k, to):
        return [
            remote(nst, nrv.at[k % 2, b], ns.at[i], nr.at[k % 2, b], {"freq": 1 - f, "base": other})
            for i, other in enumerate(to)
        ]

    def step(k, carry):
        par = k % 2
        rounded = z_s[...].astype(BF16)
        zrv[b] = rounded
        nst[...] = norm_of(rounded.astype(F32))
        n_sends = norm_copies(k, base_peers)
        z_sends = [
            remote(zrv.at[b], zrv.at[b], zs.at[i], zr.at[b], {"base": other})
            for i, other in enumerate(base_peers[:-1])
        ]
        for c in n_sends + z_sends:
            c.start()

        @pl.when(k == 0)
        def _():
            copy_a.wait()

            def turn(j, carry):
                block = pl.ds(pl.multiple_of(j * TILE, TILE), TILE)
                at_s[block, :] = a_s[:, block].T
                return carry

            lax.fori_loop(0, nb, turn, 0)

        for i, dq in enumerate(reversed(outward(nq_y))):
            y0 = (yy // 2 + dq) % nq_y * 2
            firsts = [xl * ny + y0, (1 - xl) * ny + y0]
            arrive = [firsts[0], firsts[0] + 1, firsts[1], firsts[1] + 1]
            if dq == 0:
                arrive = [firsts[0] + 1 - yy % 2, firsts[1], firsts[1] + 1]
            for t in arrive:
                local_wait(zrv.at[t], zr.at[t])
            for t0 in firsts:
                for t in (t0, t0 + 1):
                    local_wait(nrv.at[par, t], nr.at[par, t])
            for t0 in firsts:
                parts = []
                for t in (t0, t0 + 1):
                    tile = zrv[t].astype(F32)
                    parts.append((tile * factor(k, t, norm_of(tile))).astype(BF16))
                lhs = jnp.concatenate(parts, axis=1)
                these = pl.ds(pl.multiple_of(t0 * TILE, 2 * TILE), 2 * TILE)
                for n in range(0, rows, 256):
                    part = jnp.dot(lhs, at_s[these, n : n + 256], preferred_element_type=F32)
                    if i == 0 and t0 is firsts[0]:
                        acc[:, n : n + 256] = part
                    else:
                        acc[:, n : n + 256] += part

        half = nz // 2
        for z_ in range(nz):
            pst[z_ % half, z_ // half] = acc[:, TILE * z_ : TILE * z_ + TILE].astype(BF16)
        p_sends = [
            remote(
                pst.at[(zz + dz) % nz % half], prv.at[par, zz, cc], ps.at[i], pr.at[par, zz, cc],
                {"pix": (zz + dz) % nz * 2 + OWNER},
            )
            for i, dz in enumerate(outward(nz))
        ]
        for c in p_sends[:-1]:
            c.start()
        mine = zz % half
        near = [0]
        for d in range(1, half // 2 + 1):
            near += [d] if 2 * d == half else [d, -d]
        r_sends = [
            remote(rrv.at[mine], rrv.at[mine], rs.at[i], rr.at[mine], {"pix": (zz + d + nz) % nz * 2 + c_})
            for i, (d, c_) in enumerate((d, c_) for d in reversed(near) for c_ in (1 - OWNER, OWNER))
        ][:-1]

        @pl.when(cc != OWNER)
        def _():
            p_sends[-1].start()
            local_wait(rrv.at[mine], rr.at[mine])

        @pl.when(cc == OWNER)
        def _():
            total = pst[mine].astype(F32)
            for dz in reversed(outward(nz)):
                oz = (zz + dz) % nz
                for c_ in (0, 1):
                    if (dz, c_) != (0, OWNER):
                        local_wait(prv.at[par, oz, c_], pr.at[par, oz, c_])
                        total += prv[par, oz, c_].astype(F32)
            for h in range(2):
                own_y = y_s[:, pl.ds(pl.multiple_of((mine + h * half) * TILE, TILE), TILE)]
                rrv[mine, h] = (own_y - total[h]).astype(BF16)
            for c in r_sends:
                c.start()

        for i, d in enumerate(near):
            q = (zz - d + nz) % half
            if d != 0:
                local_wait(rrv.at[q], rr.at[q])
            lhs = jnp.concatenate([rrv[q, 0], rrv[q, 1]], axis=1)
            low = pl.ds(pl.multiple_of(q * TILE, TILE), TILE)
            high = pl.ds(pl.multiple_of((q + half) * TILE, TILE), TILE)
            if i < len(near) - 1:
                for n in range(nb // 2):
                    cols = slice(n * 256, n * 256 + 256)
                    rhs = jnp.concatenate([a_s[low, cols], a_s[high, cols]], axis=0)
                    part = jnp.dot(lhs, rhs, preferred_element_type=F32)
                    if i == 0:
                        gacc[n] = part
                    else:
                        gacc[n] += part

        def g_copy(i, other):
            return remote(gst.at[other], grv.at[b], gs.at[i], gr.at[b], {"base": other})

        g_pairs = [((xl + dx) % 2 * ny + (yy // 2 + dq) % nq_y * 2) for dq in outward(nq_y) for dx in (1, 0)]
        g_order = []
        for t0 in g_pairs[:-1]:
            g_order += [t0, t0 + 1]
        g_order.append(g_pairs[-1] + 1 - yy % 2)
        g_sends = [g_copy(i, other) for i, other in enumerate(g_order)]

        @pl.when(k > 0)
        def _():
            for c in g_sends:
                c.wait_send()

        batch = max(len(g_pairs) // 2, 1)
        for j in range(0, len(g_pairs), batch):
            for t0 in g_pairs[j : j + batch]:
                cols = pl.ds(pl.multiple_of(t0 * TILE, 2 * TILE), 2 * TILE)
                rhs = jnp.concatenate([a_s[low, cols], a_s[high, cols]], axis=0)
                part = jnp.dot(lhs, rhs, preferred_element_type=F32)
                if len(near) > 1:
                    part += gacc[t0 // 2]
                gst[t0] = part[:, :TILE].astype(BF16)
                gst[t0 + 1] = part[:, TILE:].astype(BF16)
            for c in g_sends[2 * j : 2 * (j + batch)]:
                c.start()
        for c in n_sends + z_sends + p_sends[:-1]:
            c.wait_send()

        @pl.when(cc != OWNER)
        def _():
            p_sends[-1].wait_send()

        @pl.when(cc == OWNER)
        def _():
            for c in r_sends:
                c.wait_send()

        x = z_s[...] * factor(k, b, norm_of(zrv[b].astype(F32)))
        total = gst[b].astype(F32)
        for other in reversed(base_peers[:-1]):
            local_wait(grv.at[other], gr.at[other])
            total += grv[other].astype(F32)
        z_s[...] = x + STRIDE * total
        return carry

    lax.fori_loop(0, ITERS, step, 0)

    for i, other in enumerate(base_peers[:-1]):
        remote(gst.at[other], grv.at[b], gs.at[i], gr.at[b], {"base": other}).wait_send()
    z = z_s[...]
    nst[...] = norm_of(z)
    (send,) = norm_copies(ITERS, [b])
    send.start()
    local_wait(nrv.at[ITERS % 2, b], nr.at[ITERS % 2, b])
    send.wait_send()
    out_ref[...] = z * factor(ITERS, b, nst[...])


def on_device(nb, npx, sensing_operator_parts, sampled_correlations, first_sky_estimate, patch_order_record):
    a = sensing_operator_parts[0]
    chans, rows = sampled_correlations.shape
    pixels = a.shape[1]
    nz = npx // 2
    dma = pltpu.SemaphoreType.DMA
    anywhere = pl.BlockSpec(memory_space=pl.ANY)
    vmem = pl.BlockSpec(memory_space=pltpu.VMEM)
    image = pl.pallas_call(
        functools.partial(kernel, nb, npx, nb * npx // 4),
        out_shape=jax.ShapeDtypeStruct((chans, TILE), F32),
        in_specs=[anywhere, anywhere, anywhere, vmem],
        out_specs=vmem,
        scratch_shapes=[
            pltpu.VMEM((rows, pixels), BF16),
            pltpu.VMEM((pixels, rows), BF16),
            pltpu.VMEM((chans, rows), F32),
            pltpu.VMEM((chans, TILE), F32),
            pltpu.VMEM((ITERS, nb, 1, TILE), F32),
            pltpu.VMEM((nb, chans, TILE), BF16),
            pltpu.VMEM((1, TILE), F32),
            pltpu.VMEM((2, nb, 1, TILE), F32),
            pltpu.VMEM((chans, rows), F32),
            pltpu.VMEM((nz // 2, 2, chans, TILE), BF16),
            pltpu.VMEM((2, nz, 2, 2, chans, TILE), BF16),
            pltpu.VMEM((nz // 2, 2, chans, TILE), BF16),
            pltpu.VMEM((nb // 2, chans, 2 * TILE), F32),
            pltpu.VMEM((nb, chans, TILE), BF16),
            pltpu.VMEM((nb, chans, TILE), BF16),
            dma((3,)),
            dma((nb,)), dma((nb,)),
            dma((nb,)), dma((2, nb)),
            dma((nz,)), dma((2, nz, 2)),
            dma((nz,)), dma((nz // 2,)),
            dma((nb,)), dma((nb,)),
        ],
        compiler_params=pltpu.CompilerParams(collective_id=0, has_side_effects=True),
        name="shrinkage",
    )(a, sampled_correlations, first_sky_estimate.reshape(chans, TILE), patch_order_record)
    return image.reshape(chans, 1, 1, TILE)


def solution(mesh):
    in_specs = (
        P("freq", "base", "pix"),
        P("freq", "base"),
        P("freq", "pix", "base", None),
        P(None, "pix"),
    )
    out_specs = P("freq", "pix", "base", None)
    return jax.shard_map(
        functools.partial(on_device, mesh.shape["base"], mesh.shape["pix"]),
        mesh=mesh, in_specs=in_specs, out_specs=out_specs, check_vma=False,
    )
```

time: 160 us -> 148 us (0.925)
  Pallas kernels: 158 us -> 147 us
    pallas_call x1, Pallas kernels: 158 us -> 147 us  [on_device(): pl.pallas_call(functools.partial(kernel, nb, npx, nb * npx // 4), out_sha...]
where the time goes in v2:
time: 148 us
  Pallas kernels  147 us (99%)
    pallas_call x1, Pallas kernels, on_device(): pl.pallas_call(functools.partial(kernel, nb, npx, nb * npx // 4), out_sha...  147 us

profile of v2, /device:TPU:8, one launch (start us, length us, event | category | flops | bytes accessed | tf_op | source)
XLA Modules:
  0.0 147.9 jit_solution(411885235747643406)
XLA Ops:
  0.0 146.6 %shrinkage.1 = f32[32,128]{1,0:T(8,128)} custom-call(bf16[1024,2048]{1,0:T(8,128)(2,1)} %bitcast.5, f32[32,1024]{1,0:T(8,128)} %y_hbm.1, f32[32,128]{1,0:T(8,128)} %bitcast.7, s32[6,16]{1,0:T(8,128)} %rank_ref.1), custom_call_target="tpu_custom_call" | custom-call | tf_op jit(solution)/shard_map/shrinkage/pallas_call | solution.py:271
  146.6 1.3 copy.7

commit v3 on v2

--- a/solution.py
+++ b/solution.py
@@ -34,7 +34,7 @@
     nb, npx, keep_count,
     a_hbm, y_hbm, x0_hbm, rank_ref, out_ref,
     a_s, at_s, y_s, z_s, keep_s,
-    zrv, nst, nrv, acc, pst, prv, rrv, gacc, gst, grv,
+    zrv, nst, nrv, acc, pst, psent, ptot, prv, rrv, gacc, gst, gsent, gtot, grv,
     in_sem, zs, zr, ns, nr, ps, pr, rs, rr, gs, gr,
 ):
     ny, nz = nb // 2, npx // 2
@@ -67,6 +67,9 @@
         row = jnp.broadcast_to(rank_ref[k : k + 1, :], (nb, nb))
         column = jnp.sum(jnp.where(same & (row < keep_count), 1.0, 0.0), axis=1, keepdims=True)
         keep_s[k] = jnp.broadcast_to(column, (nb, TILE)).reshape(nb, 1, TILE)
+
+    for ref in (psent, ptot, gsent, gtot):
+        ref[...] = jnp.zeros_like(ref)
 
     copy_x0.wait()
     copy_y.wait()
@@ -144,7 +147,8 @@
 
         half = nz // 2
         for z_ in range(nz):
-            pst[z_ % half, z_ // half] = acc[:, TILE * z_ : TILE * z_ + TILE].astype(BF16)
+            at = z_ % half, z_ // half
+            pst[at] = (acc[:, TILE * z_ : TILE * z_ + TILE] - psent[at]).astype(BF16)
         p_sends = [
             remote(
                 pst.at[(zz + dz) % nz % half], prv.at[par, zz, cc], ps.at[i], pr.at[par, zz, cc],
@@ -154,6 +158,7 @@
         ]
         for c in p_sends[:-1]:
             c.start()
+        psent[...] += pst[...].astype(F32)
         mine = zz % half
         near = [0]
         for d in range(1, half // 2 + 1):
@@ -170,13 +175,14 @@
 
         @pl.when(cc == OWNER)
         def _():
-            total = pst[mine].astype(F32)
+            total = ptot[...] + pst[mine].astype(F32)
             for dz in reversed(outward(nz)):
                 oz = (zz + dz) % nz
                 for c_ in (0, 1):
                     if (dz, c_) != (0, OWNER):
                         local_wait(prv.at[par, oz, c_], pr.at[par, oz, c_])
                         total += prv[par, oz, c_].astype(F32)
+            ptot[...] = total
             for h in range(2):
                 own_y = y_s[:, pl.ds(pl.multiple_of((mine + h * half) * TILE, TILE), TILE)]
                 rrv[mine, h] = (own_y - total[h]).astype(BF16)
@@ -223,8 +229,8 @@
                 part = jnp.dot(lhs, rhs, preferred_element_type=F32)
                 if len(near) > 1:
                     part += gacc[t0 // 2]
-                gst[t0] = part[:, :TILE].astype(BF16)
-                gst[t0 + 1] = part[:, TILE:].astype(BF16)
+                gst[t0] = (part[:, :TILE] - gsent[t0]).astype(BF16)
+                gst[t0 + 1] = (part[:, TILE:] - gsent[t0 + 1]).astype(BF16)
             for c in g_sends[2 * j : 2 * (j + batch)]:
                 c.start()
         for c in n_sends + z_sends + p_sends[:-1]:
@@ -239,11 +245,13 @@
             for c in r_sends:
                 c.wait_send()
 
+        gsent[...] += gst[...].astype(F32)
         x = z_s[...] * factor(k, b, norm_of(zrv[b].astype(F32)))
-        total = gst[b].astype(F32)
+        total = gtot[...] + gst[b].astype(F32)
         for other in reversed(base_peers[:-1]):
             local_wait(grv.at[other], gr.at[other])
             total += grv[other].astype(F32)
+        gtot[...] = total
         z_s[...] = x + STRIDE * total
         return carry
 
@@ -284,10 +292,14 @@
             pltpu.VMEM((2, nb, 1, TILE), F32),
             pltpu.VMEM((chans, rows), F32),
             pltpu.VMEM((nz // 2, 2, chans, TILE), BF16),
+            pltpu.VMEM((nz // 2, 2, chans, TILE), F32),
+            pltpu.VMEM((2, chans, TILE), F32),
             pltpu.VMEM((2, nz, 2, 2, chans, TILE), BF16),
             pltpu.VMEM((nz // 2, 2, chans, TILE), BF16),
             pltpu.VMEM((nb // 2, chans, 2 * TILE), F32),
             pltpu.VMEM((nb, chans, TILE), BF16),
+            pltpu.VMEM((nb, chans, TILE), F32),
+            pltpu.VMEM((chans, TILE), F32),
             pltpu.VMEM((nb, chans, TILE), BF16),
             dma((3,)),
             dma((nb,)), dma((nb,)),

time: 148 us -> 149 us (level)
  no operation moved by 1% of the time
where the time goes in v3:
time: 149 us; the launch traced here: 148 us
  Pallas kernels  147 us (99%)
    pallas_call x1, Pallas kernels, on_device(): pl.pallas_call(functools.partial(kernel, nb, npx, nb * npx // 4), out_sha...  147 us

profile of v3, /device:TPU:8, one launch (start us, length us, event | category | flops | bytes accessed | tf_op | source)
XLA Modules:
  0.0 148.2 jit_solution(1109470991625632321)
XLA Ops:
  0.0 146.9 %shrinkage.1 = f32[32,128]{1,0:T(8,128)} custom-call(bf16[1024,2048]{1,0:T(8,128)(2,1)} %bitcast.5, f32[32,1024]{1,0:T(8,128)} %y_hbm.1, f32[32,128]{1,0:T(8,128)} %bitcast.7, s32[6,16]{1,0:T(8,128)} %rank_ref.1), custom_call_target="tpu_custom_call" | custom-call | tf_op jit(solution)/shard_map/shrinkage/pallas_call | solution.py:279
  146.9 1.3 copy.7

commit v4 on v3

--- a/solution.py
+++ b/solution.py
@@ -106,7 +106,13 @@
             remote(zrv.at[b], zrv.at[b], zs.at[i], zr.at[b], {"base": other})
             for i, other in enumerate(base_peers[:-1])
         ]
-        for c in n_sends + z_sends:
+
+        @pl.when(k > 0)
+        def _():
+            for c in n_sends:
+                c.start()
+
+        for c in z_sends:
             c.start()
 
         @pl.when(k == 0)
@@ -128,9 +134,13 @@
                 arrive = [firsts[0] + 1 - yy % 2, firsts[1], firsts[1] + 1]
             for t in arrive:
                 local_wait(zrv.at[t], zr.at[t])
-            for t0 in firsts:
-                for t in (t0, t0 + 1):
-                    local_wait(nrv.at[par, t], nr.at[par, t])
+
+            @pl.when(k > 0)
+            def _():
+                for t0 in firsts:
+                    for t in (t0, t0 + 1):
+                        local_wait(nrv.at[par, t], nr.at[par, t])
+
             for t0 in firsts:
                 parts = []
                 for t in (t0, t0 + 1):
@@ -233,8 +243,13 @@
                 gst[t0 + 1] = (part[:, TILE:] - gsent[t0 + 1]).astype(BF16)
             for c in g_sends[2 * j : 2 * (j + batch)]:
                 c.start()
-        for c in n_sends + z_sends + p_sends[:-1]:
+        for c in z_sends + p_sends[:-1]:
             c.wait_send()
+
+        @pl.when(k > 0)
+        def _():
+            for c in n_sends:
+                c.wait_send()
 
         @pl.when(cc != OWNER)
         def _():

time: 149 us -> 148 us (level)
  no operation moved by 1% of the time
where the time goes in v4:
time: 148 us
  Pallas kernels  146 us (99%)
    pallas_call x1, Pallas kernels, on_device(): pl.pallas_call(functools.partial(kernel, nb, npx, nb * npx // 4), out_sha...  146 us

profile of v4, /device:TPU:8, one launch (start us, length us, event | category | flops | bytes accessed | tf_op | source)
XLA Modules:
  0.0 147.8 jit_solution(13242748341818750578)
XLA Ops:
  0.0 146.5 %shrinkage.1 = f32[32,128]{1,0:T(8,128)} custom-call(bf16[1024,2048]{1,0:T(8,128)(2,1)} %bitcast.5, f32[32,1024]{1,0:T(8,128)} %y_hbm.1, f32[32,128]{1,0:T(8,128)} %bitcast.7, s32[6,16]{1,0:T(8,128)} %rank_ref.1), custom_call_target="tpu_custom_call" | custom-call | tf_op jit(solution)/shard_map/shrinkage/pallas_call | solution.py:294
  146.5 1.3 copy.7
